TPU v7x, 64 devices: a 2x2x8 block of a 4x4x8 slice. The times are simulated.
64 devices in a mesh: rep: 4 (over x, y), dp: 16 (over z, core).
Axes of the slice: x: 2, y: 2, z: 8, core: 2. Of those that a mesh axis runs over, the one named last changes fastest.
The devices are a block of a 4x4x8 slice.
Arguments:
- x: bfloat16 [64, 4096, 512], P(('rep', 'dp')), parts along dimension 0
- dy: bfloat16 [64, 4096, 512], P(('rep', 'dp')), parts along dimension 0
- w_gate: bfloat16 [2, 512, 1280], P(None, 'dp')
- w_up: bfloat16 [2, 512, 1280], P(None, 'dp')
- w_down: bfloat16 [2, 1280, 512], P(None, 'dp')
- m_w_gate: float32 [2, 512, 1280], P(None, 'dp')
- m_w_up: float32 [2, 512, 1280], P(None, 'dp')
- m_w_down: float32 [2, 1280, 512], P(None, 'dp')
- v_w_gate: float32 [2, 512, 1280], P(None, 'dp')
- v_w_up: float32 [2, 512, 1280], P(None, 'dp')
- v_w_down: float32 [2, 1280, 512], P(None, 'dp')
Outputs:
- output 1: bfloat16 [8, 512, 1280], P('rep', 'dp'), parts along dimension 0
- output 2: bfloat16 [8, 512, 1280], P('rep', 'dp'), parts along dimension 0
- output 3: bfloat16 [8, 1280, 512], P('rep', 'dp'), parts along dimension 0
- output 4: float32 [8, 512, 1280], P('rep', 'dp'), parts along dimension 0
- output 5: float32 [8, 512, 1280], P('rep', 'dp'), parts along dimension 0
- output 6: float32 [8, 1280, 512], P('rep', 'dp'), parts along dimension 0
- output 7: float32 [8, 512, 1280], P('rep', 'dp'), parts along dimension 0
- output 8: float32 [8, 512, 1280], P('rep', 'dp'), parts along dimension 0
- output 9: float32 [8, 1280, 512], P('rep', 'dp'), parts along dimension 0
There are 4 independent parts. A program takes and returns all parts, laid end to end along the dimension named above; an argument that names none is the same for every part.
All inputs are finite; a program needn't handle non-finite values.
Results may differ from a plain program's by a relative error of at most 0.0222.
Values are sent between devices in bfloat16 or wider.
A program may use at most 768 MiB of HBM per device.

v0:
```python
import functools

import jax
import jax.numpy as jnp
from jax import lax
from jax.experimental import pallas as pl
from jax.experimental.pallas import tpu as pltpu
from jax.sharding import PartitionSpec as P

MESH = pl.DeviceIdType.MESH
BF, F32 = jnp.bfloat16, jnp.float32
VMEM_LIMIT = 66_500_000
TILE = 512
WIDE = 1024
COLS = 256


def dot(a, b):
    return jnp.dot(a, b, preferred_element_type=F32)


def dot_t(a, b):
    return lax.dot_general(a, b, (((0,), (0,)), ((), ())), preferred_element_type=F32)


def norm_scale(wide):
    return lax.rsqrt(jnp.mean(wide * wide, -1, keepdims=True) + 1e-6)


def places(n):
    nz = n // 2
    me = lax.axis_index("dp")
    z, core = me // 2, me % 2
    return me, z, core, ((z + 1) % nz) * 2 + core, ((z + nz - 1) % nz) * 2 + core, me + 1 - 2 * core


def barrier(devices):
    sem = pltpu.get_barrier_semaphore()
    for device in devices:
        pl.semaphore_signal(sem, inc=1, device_id={"dp": device}, device_id_type=MESH)
    pl.semaphore_wait(sem, len(devices))


def forward_kernel(n, x_hbm, wg_ref, wu_ref, wd_ref, h1_hbm, a1_hbm, hid_hbm, a0_hbm, gu_hbm, dt_hbm,
                   x, a0, hid, gu, d, dt, send_sem, recv_sem, in_sem, out_sem):
    nz = n // 2
    me, z, core, right, left, partner = places(n)
    tokens = x.shape[0]
    steps = tokens // TILE
    load = pltpu.make_async_copy(x_hbm, x, in_sem)
    load.start()
    barrier((right, left, partner))

    more, less = nz // 2, nz - 1 - nz // 2
    parts = [
        (wg_ref.at[0], gu, 0, more, less),
        (wu_ref.at[0], gu, 1, less, more),
        (wd_ref.at[0], d, 0, more, less),
        (wg_ref.at[1], gu, 2, less, more),
        (wu_ref.at[1], gu, 3, more, less),
        (wd_ref.at[1], d, 1, less, more),
    ]
    sent = []

    def block(i, chip, which):
        src, whole, first = parts[i][:3]
        rows = src.shape[0]
        return whole.at[first, pl.ds(pl.multiple_of((chip * 2 + which) * rows, 16), rows), :]

    def copy(i, k, src, dst, device):
        return pltpu.make_async_remote_copy(
            src_ref=src, dst_ref=dst, send_sem=send_sem.at[i, k], recv_sem=recv_sem.at[i, k],
            device_id={"dp": device}, device_id_type=MESH,
        )

    def send(i, k, src, dst, device):
        c = copy(i, k, src, dst, device)
        c.start()
        sent.append(c)

    def arrived(i, k, at):
        copy(i, k, at, at, partner).wait_recv()

    def begin(i):
        src, whole, first = parts[i][:3]
        rows = src.shape[0]
        own = block(i, z, core)
        send(i, 0, src, own, right)
        send(i, more, src, own, left)
        send(i, 2 * more, src, own, partner)
        whole[first, pl.ds(pl.multiple_of(me * rows, 16), rows), :] = src[...]

    def relay(i, s):
        hops_right, hops_left = parts[i][3:]
        if s <= hops_right:
            at = block(i, (z + nz - s) % nz, core)
            arrived(i, s - 1, at)
            if s < hops_right:
                send(i, s, at, at, right)
            send(i, 2 * more + s, at, at, partner)
        if s <= hops_left:
            at = block(i, (z + s) % nz, core)
            arrived(i, more + s - 1, at)
            if s < hops_left:
                send(i, more + s, at, at, left)
            send(i, 3 * more + s, at, at, partner)

    def finish(i):
        hops_right, hops_left = parts[i][3:]
        arrived(i, 2 * more, block(i, z, 1 - core))
        for s in range(1, hops_right + 1):
            arrived(i, 2 * more + s, block(i, (z + nz - s) % nz, 1 - core))
        for s in range(1, hops_left + 1):
            arrived(i, 3 * more + s, block(i, (z + s) % nz, 1 - core))

    outs = []

    def store(k, src, dst):
        c = pltpu.make_async_copy(src, dst, out_sem.at[k])
        c.start()
        outs.append(c)

    for i in range(3):
        begin(i)
    load.wait()

    def norm_step(t, _):
        at = pl.ds(pl.multiple_of(t * TILE, TILE), TILE)
        wide = x[at, :].astype(F32)
        a0[at, :] = (wide * norm_scale(wide)).astype(BF)
        return 0

    with jax.named_scope("gather0"):
        for s in range(1, more):
            if s < 3:
                lax.fori_loop((s - 1) * (steps // 2), s * (steps // 2), norm_step, 0)
            for i in range(3):
                relay(i, s)
        for i in range(3, 6):
            begin(i)
        relay(0, more)
        relay(1, more)
        finish(0)
        finish(1)
    store(0, a0, a0_hbm)

    def up_step(t, _):
        at = pl.ds(pl.multiple_of(t * TILE, TILE), TILE)
        a = a0[at, :]
        gate = dot(a, gu[0])
        up = dot(a, gu[1])
        hid[at, :] = (gate * jax.nn.sigmoid(gate) * up).astype(BF)
        return 0

    def down_step(t, _):
        at = pl.ds(pl.multiple_of(t * TILE, TILE), TILE)
        h = x[at, :] + dot(hid[at, :], d[0]).astype(BF)
        x[at, :] = h
        wide = h.astype(F32)
        a0[at, :] = (wide * norm_scale(wide)).astype(BF)
        return 0

    moves = [(2, 4), (3, 1), (4, 1), (5, 1), (3, 2), (4, 2), (5, 2), (3, 3), (4, 3), (5, 3), None, (3, 4), None, (4, 4), None, (5, 4)]
    each = steps // 8
    for q in range(8):
        with jax.named_scope("up"):
            lax.fori_loop(q * each, (q + 1) * each, up_step, 0)
        with jax.named_scope("move"):
            relay(*moves[q])
    store(1, hid, hid_hbm)
    store(2, gu.at[pl.ds(0, 2)], gu_hbm.at[pl.ds(0, 2)])
    outs[0].wait()
    finish(2)
    for q in range(8):
        with jax.named_scope("down"):
            lax.fori_loop(q * each, (q + 1) * each, down_step, 0)
        with jax.named_scope("move"):
            if moves[8 + q] is not None:
                relay(*moves[8 + q])
        at = pl.ds(q * each * TILE, each * TILE)
        store(6 + 2 * q, x.at[at, :], h1_hbm.at[at, :])
        store(7 + 2 * q, a0.at[at, :], a1_hbm.at[at, :])
        if q == 0:
            dt[0] = d[0].T
            store(3, dt.at[0], dt_hbm.at[0])
    with jax.named_scope("finish"):
        finish(3)
        finish(4)
    store(5, gu.at[pl.ds(2, 2)], gu_hbm.at[pl.ds(2, 2)])
    finish(5)
    dt[1] = d[1].T
    store(4, dt.at[1], dt_hbm.at[1])
    for c in sent:
        c.wait_send()
    for c in outs[1:]:
        c.wait()


def forward(n, x, wg, wu, wd):
    tokens, dim = x.shape
    hidden = wg.shape[2]
    anyspace, vmem = pl.BlockSpec(memory_space=pl.ANY), pl.BlockSpec(memory_space=pltpu.VMEM)
    shapes = [(tokens, dim), (tokens, dim), (tokens, hidden), (tokens, dim), (4, dim, hidden), (2, dim, hidden)]
    sems = 4 * (n // 4) + 1
    return pl.pallas_call(
        functools.partial(forward_kernel, n),
        out_shape=[jax.ShapeDtypeStruct(s, BF) for s in shapes],
        in_specs=[anyspace, vmem, vmem, vmem],
        out_specs=[anyspace] * 6,
        scratch_shapes=[
            pltpu.VMEM((tokens, dim), BF),
            pltpu.VMEM((tokens, dim), BF),
            pltpu.VMEM((tokens, hidden), BF),
            pltpu.VMEM((4, dim, hidden), BF),
            pltpu.VMEM((2, hidden, dim), BF),
            pltpu.VMEM((2, dim, hidden), BF),
            pltpu.SemaphoreType.DMA((6, sems)),
            pltpu.SemaphoreType.DMA((6, sems)),
            pltpu.SemaphoreType.DMA,
            pltpu.SemaphoreType.DMA((22,)),
        ],
        compiler_params=pltpu.CompilerParams(collective_id=0, has_side_effects=True, vmem_limit_bytes=VMEM_LIMIT),
        cost_estimate=pl.CostEstimate(flops=6 * tokens * dim * hidden, bytes_accessed=40 << 20, transcendentals=0),
        name="forward0",
    )(x, wg, wu, wd)


def backward_kernel(n, h1_hbm, a1_hbm, dy_hbm, a0_hbm, hid_hbm, gu_hbm, dt_hbm, out_gu, out_d, factor,
                    h1, a, dh, acc, gu, gt, dt, hid, tgu, td, pgu, pd, rgu, rd, sum_gu, sum_d, acc_gu, acc_d, ssq, all_ssq,
                    in_sem, hid_sem, p_send, p_recv, send_gu, recv_gu, send_d, recv_d, q_send, q_recv):
    nz = n // 2
    me, z, core, right, left, partner = places(n)
    tokens, dim = a.shape
    hidden = dt.shape[1]
    nf = hidden // COLS
    far, near = nz // 2, nz - 1 - nz // 2
    rows_g, rows_d = dim // n, hidden // n
    tiles, slots = tokens // TILE, hid.shape[0]
    half = tokens // WIDE // 2

    def load(k, src, dst):
        return pltpu.make_async_copy(src, dst, in_sem.at[k])

    def load_hid(t):
        slot = t % slots
        return pltpu.make_async_copy(hid_hbm.at[pl.ds(pl.multiple_of(t * TILE, TILE), TILE), :], hid.at[slot], hid_sem.at[slot])

    half_t = tokens // 2
    lo_t, hi_t = pl.ds(0, half_t), pl.ds(half_t, half_t)
    early = [
        load(0, gu_hbm.at[pl.ds(2, 2)], gu),
        load(1, dt_hbm.at[1], dt),
        load(2, a1_hbm.at[lo_t, :], a.at[lo_t, :]),
        load(3, dy_hbm.at[lo_t, :], dh.at[lo_t, :]),
    ]
    soon = [load(4, a1_hbm.at[hi_t, :], a.at[hi_t, :]), load(5, dy_hbm.at[hi_t, :], dh.at[hi_t, :])]
    whole_h1 = load(6, h1_hbm, h1)
    later = [load(7, a0_hbm, a), load(8, gu_hbm.at[pl.ds(0, 2)], gu), load(9, dt_hbm.at[0], dt)]
    for c in early:
        c.start()

    sem = pltpu.get_barrier_semaphore()
    for k in range(1, n):
        pl.semaphore_signal(sem, inc=1, device_id={"dp": (me + k) % n}, device_id_type=MESH)
    pl.semaphore_wait(sem, n - 1)

    ssq[...] = jnp.zeros_like(ssq)

    def begin_step(t, _):
        acc[pl.ds(pl.multiple_of(t * TILE, TILE), TILE), :] = jnp.zeros((TILE, dim), F32)
        return 0

    lax.fori_loop(0, tiles, begin_step, 0)
    early[0].wait()
    for j in range(nf):
        for i in range(2):
            gt[j, i * COLS : (i + 1) * COLS, :] = gu[i, :, j * COLS : (j + 1) * COLS].T
    for c in early[1:]:
        c.wait()
    for c in soon:
        c.start()

    def over_gu(q):
        return pltpu.make_async_remote_copy(
            src_ref=tgu.at[q, :, :, 1 - core], dst_ref=pgu.at[q], send_sem=p_send.at[q], recv_sem=p_recv.at[q],
            device_id={"dp": partner}, device_id_type=MESH,
        )

    def over_d(layer):
        k = 2 * nf + layer
        return pltpu.make_async_remote_copy(
            src_ref=td.at[layer, :, 1 - core], dst_ref=pd.at[layer], send_sem=p_send.at[k], recv_sem=p_recv.at[k],
            device_id={"dp": partner}, device_id_type=MESH,
        )

    def sides(odd):
        sign = 1 - 2 * odd

        def chip(way, s):
            return (z + 2 * nz + sign * (far - s)) % nz if way == 0 else (z + 2 * nz - sign * (near - s)) % nz

        def device(way):
            return ((z + nz + (sign if way == 0 else -sign)) % nz) * 2 + core

        return chip, device

    def squared(v):
        g = v.astype(F32)
        g = g * g
        while g.ndim > 2:
            g = jnp.sum(g, axis=0)
        g = jnp.sum(g, axis=0, keepdims=True)
        total = g[:, 0:128]
        for k in range(1, g.shape[1] // 128):
            total = total + g[:, k * 128 : (k + 1) * 128]
        ssq[0:1, :] += total

    class Gu:
        def __init__(self, q):
            self.q = q
            self.chip, self.device = sides(q % 2)

        def over(self):
            return over_gu(self.q)

        def term(self, b):
            return tgu[self.q, :, b, core].astype(F32) + pgu[self.q, :, b].astype(F32)

        def keep(self, b, v):
            tgu[self.q, :, b, core] = v

        def got(self, way, s):
            return rgu[self.q, way, s].astype(F32)

        def move(self, way, s):
            return pltpu.make_async_remote_copy(
                src_ref=tgu.at[self.q, :, self.chip(way, s), core], dst_ref=rgu.at[self.q, way, s],
                send_sem=send_gu.at[self.q, way, s], recv_sem=recv_gu.at[self.q, way, s],
                device_id={"dp": self.device(way)}, device_id_type=MESH,
            )

        def put(self, v):
            layer, j = 1 - self.q // nf, self.q % nf
            sum_gu[layer, :, :, pl.ds(pl.multiple_of(j * COLS, COLS), COLS)] = v

    class Down:
        def __init__(self, layer):
            self.layer = layer
            self.chip, self.device = sides(layer)

        def over(self):
            return over_d(self.layer)

        def term(self, b):
            return td[self.layer, b, core].astype(F32) + pd[self.layer, b].astype(F32)

        def keep(self, b, v):
            td[self.layer, b, core] = v

        def got(self, way, s):
            return rd[self.layer, way, s].astype(F32)

        def move(self, way, s):
            return pltpu.make_async_remote_copy(
                src_ref=td.at[self.layer, self.chip(way, s), core], dst_ref=rd.at[self.layer, way, s],
                send_sem=send_d.at[self.layer, way, s], recv_sem=recv_d.at[self.layer, way, s],
                device_id={"dp": self.device(way)}, device_id_type=MESH,
            )

        def put(self, v):
            sum_d[self.layer] = v

    def event(part, s):
        def on(way):
            b = part.chip(way, s)
            part.move(way, s - 1).wait()
            part.keep(b, (part.got(way, s - 1) + part.term(b)).astype(BF))
            part.move(way, s).start()

        @pl.when(s == 0)
        def _():
            part.over().wait()
            for way in range(2):
                b = part.chip(way, s)
                part.keep(b, part.term(b).astype(BF))
            for way in range(2):
                part.move(way, s).start()

        @pl.when(jnp.logical_and(s > 0, s < far))
        def _():
            on(0)

        @pl.when(jnp.logical_and(s > 0, s < near))
        def _():
            on(1)

        @pl.when(s == far)
        def _():
            part.move(0, far - 1).wait()
            part.move(1, near - 1).wait()
            v = (part.term(z) + part.got(0, far - 1) + part.got(1, near - 1)).astype(BF)
            part.put(v)
            squared(v)

    first_top, first_down, first_low = 0, 2 * nf, 2 * nf + 2
    end_low = first_low + 2 * nf

    def ready(q):
        return 2 * (q + q // nf)

    def events(p):
        def each_gu(q, _):
            s = p - (ready(q) + 2)

            @pl.when(jnp.logical_and(s >= 0, s <= far))
            def _():
                event(Gu(q), s)

            return 0

        def each_d(k, _):
            s = p - (first_down + 2 * k)

            @pl.when(jnp.logical_and(s >= 0, s <= far))
            def _():
                event(Down(1 - k), s)

            return 0

        @pl.when(jnp.logical_and(p >= first_down, p < first_down + far + 3))
        def _():
            lax.fori_loop(0, 2, each_d, 0)

        lax.fori_loop(0, 2 * nf, each_gu, 0)

    def grads(q):
        for b in range(nz):
            for c in range(2):
                k = (b * 2 + c) * rows_g
                for i in range(2):
                    tgu[q, i, b, c] = acc_gu[k : k + rows_g, i * COLS : (i + 1) * COLS].astype(BF)
        over_gu(q).start()

    def wide_step(j, with_top):
        cols = pl.ds(pl.multiple_of(j * COLS, COLS), COLS)

        def body(t, _):
            at = pl.ds(pl.multiple_of(t * WIDE, WIDE), WIDE)
            rows = a[at, :]
            by_y = dh[at, :]
            gate = dot(rows, gu[0, :, cols])
            up = dot(rows, gu[1, :, cols])
            by_hid = dot(by_y, dt[:, cols]).astype(BF).astype(F32)
            sig = jax.nn.sigmoid(gate)
            act = gate * sig
            by_up = (by_hid * act).astype(BF)
            by_gate = (by_hid * up * (sig + act * (1.0 - sig))).astype(BF)
            by_both = jnp.concatenate([by_gate, by_up], axis=1)
            acc_gu[...] += dot_t(rows, by_both)
            if with_top:
                acc_d[...] += dot_t(by_y, (act * up).astype(BF))
                acc[at, :] += dot(by_both, gt[j])
            return 0

        return body

    def top_end(t, _):
        at = pl.ds(pl.multiple_of(t * TILE, TILE), TILE)
        wide = h1[at, :].astype(F32)
        scale = norm_scale(wide)
        by_a = acc[at, :].astype(BF).astype(F32)
        by_h = scale * by_a - wide * (scale * scale * scale * jnp.mean(by_a * wide, -1, keepdims=True))
        dh[at, :] = dh[at, :] + by_h.astype(BF)
        return 0

    def down_step(t, _):
        load_hid(t).wait()
        acc[0:hidden, :] += dot_t(hid[t % slots], dh[pl.ds(pl.multiple_of(t * TILE, TILE), TILE), :])

        @pl.when(t + slots < tiles)
        def _():
            load_hid(t + slots).start()

        return 0

    def zero():
        acc_gu[...] = jnp.zeros_like(acc_gu)

    def phase(p, _):
        part_of = p % 2
        lo = part_of * half

        @pl.when(p < first_down)
        def _():
            j = p // 2

            @pl.when(p == 1)
            def _():
                for c in soon:
                    c.wait()
                whole_h1.start()
                for t in range(slots):
                    load_hid(t).start()

            @pl.when(part_of == 0)
            def _():
                zero()
                acc_d[...] = jnp.zeros_like(acc_d)

            with jax.named_scope("top"):
                lax.fori_loop(lo, lo + half, wide_step(j, True), 0)

            @pl.when(part_of == 1)
            def _():
                grads(j)
                down = acc_d[...].T.astype(BF)
                for i in range(COLS // 16):
                    row = j * COLS + i * 16
                    device = row // rows_d
                    td[1, device // 2, device % 2, pl.ds(pl.multiple_of(row % rows_d, 16), 16), :] = down[i * 16 : i * 16 + 16, :]

            @pl.when(p == first_down - 1)
            def _():
                over_d(1).start()
                for c in later:
                    c.start()
                whole_h1.wait()
                with jax.named_scope("topend"):
                    lax.fori_loop(0, tiles, top_end, 0)

        @pl.when(jnp.logical_and(p >= first_down, p < first_low))
        def _():
            @pl.when(part_of == 0)
            def _():
                acc[0:hidden, :] = jnp.zeros((hidden, dim), F32)

            lax.fori_loop(part_of * (tiles // 2), part_of * (tiles // 2) + tiles // 2, down_step, 0)

            @pl.when(part_of == 1)
            def _():
                for b in range(nz):
                    for c in range(2):
                        k = (b * 2 + c) * rows_d
                        td[0, b, c] = acc[k : k + rows_d, :].astype(BF)
                over_d(0).start()
                for c in later:
                    c.wait()

        @pl.when(jnp.logical_and(p >= first_low, p < end_low))
        def _():
            j = (p - first_low) // 2

            @pl.when(part_of == 0)
            def _():
                zero()

            with jax.named_scope("low"):
                lax.fori_loop(lo, lo + half, wide_step(j, False), 0)

            @pl.when(part_of == 1)
            def _():
                grads(nf + j)

        with jax.named_scope("events"):
            events(p)
        return 0

    lax.fori_loop(0, end_low + far + 1, phase, 0)
    results = [
        pltpu.make_async_copy(sum_gu, out_gu, in_sem.at[0]),
        pltpu.make_async_copy(sum_d, out_d, in_sem.at[1]),
    ]
    for c in results:
        c.start()

    all_ssq[me] = ssq[...]

    def scalar(k, slot):
        return pltpu.make_async_remote_copy(
            src_ref=ssq, dst_ref=all_ssq.at[slot], send_sem=q_send.at[k], recv_sem=q_recv.at[k],
            device_id={"dp": (me + k) % n}, device_id_type=MESH,
        )

    def tell(k, _):
        scalar(k, me).start()
        return 0

    lax.fori_loop(1, n, tell, 0)

    def told(k, _):
        scalar(k, (me + n - k) % n).wait()
        return 0

    with jax.named_scope("told"):
        lax.fori_loop(1, n, told, 0)
    for c in results:
        c.wait()
    total = jnp.sum(jnp.sum(jnp.sum(all_ssq[...], axis=0), axis=0, keepdims=True), axis=1, keepdims=True)
    count = 3 * 2 * dim * hidden
    factor[0, 0] = jnp.max(jnp.minimum(1.0, 0.5 * lax.rsqrt(total / count + 1e-30)))


def backward(n, h1, a1, dy, a0, hid, gu, dt):
    nz = n // 2
    tokens, dim = a0.shape
    hidden = dt.shape[2]
    nf, far = hidden // COLS, nz // 2
    rg, rd = dim // n, hidden // n
    anyspace = pl.BlockSpec(memory_space=pl.ANY)
    V = lambda *s: pltpu.VMEM(s, BF)
    W = lambda *s: pltpu.VMEM(s, F32)
    S = lambda *s: pltpu.SemaphoreType.DMA(s)
    return pl.pallas_call(
        functools.partial(backward_kernel, n),
        out_shape=[
            jax.ShapeDtypeStruct((2, 2, rg, hidden), BF),
            jax.ShapeDtypeStruct((2, rd, dim), BF),
            jax.ShapeDtypeStruct((1, 1), F32),
        ],
        in_specs=[anyspace] * 7,
        out_specs=[anyspace, anyspace, pl.BlockSpec(memory_space=pltpu.SMEM)],
        scratch_shapes=[
            V(tokens, dim),
            V(tokens, dim),
            V(tokens, dim),
            W(tokens, dim),
            V(2, dim, hidden),
            V(nf, 2 * COLS, dim),
            V(dim, hidden),
            V(3, TILE, hidden),
            V(2 * nf, 2, nz, 2, rg, COLS),
            V(2, nz, 2, rd, dim),
            V(2 * nf, 2, nz, rg, COLS),
            V(2, nz, rd, dim),
            V(2 * nf, 2, far, 2, rg, COLS),
            V(2, 2, far, rd, dim),
            V(2, 2, rg, hidden),
            V(2, rd, dim),
            W(dim, 2 * COLS),
            W(dim, COLS),
            W(8, 128),
            W(n, 8, 128),
            S(10),
            S(3),
            S(2 * nf + 2),
            S(2 * nf + 2),
            S(2 * nf, 2, far),
            S(2 * nf, 2, far),
            S(2, 2, far),
            S(2, 2, far),
            S(n),
            S(n),
        ],
        compiler_params=pltpu.CompilerParams(collective_id=1, has_side_effects=True, vmem_limit_bytes=61_000_000),
        cost_estimate=pl.CostEstimate(flops=28 * tokens * dim * hidden, bytes_accessed=40 << 20, transcendentals=0),
        name="backward",
    )(h1, a1, dy, a0, hid, gu, dt)


def adamw(w, m, v, g):
    m = 0.9 * m + 0.1 * g
    v = 0.95 * v + 0.05 * g * g
    step = m * lax.rsqrt(v + 1e-8) + 0.1 * w
    return (w - 0.02 * step).astype(BF), m, v


def solution(mesh):
    n = mesh.shape["dp"]

    def step(x, dy, *arrays):
        weights, m, v = (arrays[i : i + 3] for i in (0, 3, 6))
        h1, a1, hid, a0, gu, dt = forward(n, x[0], *weights)
        sum_gu, sum_d, factor = backward(n, h1, a1, dy[0], a0, hid, gu, dt)
        gradients = [sum_gu[:, 0].astype(F32), sum_gu[:, 1].astype(F32), sum_d.astype(F32)]
        factor = factor[0, 0]
        new = [adamw(w.astype(F32), m, v, g * factor) for w, m, v, g in zip(weights, m, v, gradients, strict=True)]
        return tuple(one[which] for which in range(3) for one in new)

    states, cut = P(("rep", "dp"), None, None), P(None, "dp", None)
    return jax.shard_map(
        step,
        mesh=mesh,
        in_specs=(states, states) + (cut,) * 9,
        out_specs=(P("rep", "dp", None),) * 9,
        check_vma=False,
    )
```

profile of v0, /device:TPU:21, one launch (start us, length us, event | category | flops | bytes accessed | tf_op | source)
XLA Modules:
  0.0 210.4 jit_solution(223962693680831688)
XLA Ops:
  0.6 56.9 %forward0.1 = (bf16[4096,512]{1,0:T(8,128)(2,1)}, bf16[4096,512]{1,0:T(8,128)(2,1)}, bf16[4096,1280]{1,0:T(8,128)(2,1)}, bf16[4096,512]{1,0:T(8,128)(2,1)}, bf16...) custom-call(bf16[4096,512]{1,0:T(8,128)(2,1)} %bitcast.25, bf16[2,32,1280]{2,1,0:T(8,128)(2,1)} %wg_ref.1, ...), custom_call_target="tpu_custom_call" | custom-call | flops 16106127360 | bytes 41943040 | tf_op jit(solution)/shard_map/forward0/pallas_call | solution.py:205
  57.5 0.0 copy-start
  57.5 0.0 copy-start.1
  57.5 0.0 copy-start.6
  57.6 0.0 copy-start.2
  57.6 0.0 copy-start.3
  57.6 0.0 copy-start.4
  57.6 0.0 copy-start.5
  57.6 0.0 copy-start.7
  57.6 0.0 copy-start.8
  57.6 147.1 %backward.1 = (bf16[2,2,32,1280]{3,2,1,0:T(8,128)(2,1)}, bf16[2,80,512]{2,1,0:T(8,128)(2,1)}, f32[1,1]{1,0:T(1,128)}) custom-call(bf16[4096,512]{1,0:T(8,128)(2,1)} %get-tuple-element.18.h1_hbm, bf16[4096,512]{1,0:T(8,128)(2,1)} %get-tuple-element.19.a1_hbm, bf16[4096,512]{1,0:T(8,128)(2,1)} %bitcast.26, bf16[4096,512]{1,0:T(8,128)(2,1)} %get-tuple-element.20.a0_hbm, ...), custom_call_target="tpu_custom_call" | custom-call | flops 75161927680 | bytes 41943040 | tf_op jit(solution)/shard_map/backward/pallas_call | solution.py:613
  204.7 0.0 copy-done
  204.7 0.0 copy-done.1
  204.7 0.0 copy-done.6
  204.7 2.6 %fusion.8 = (bf16[2,80,512]{2,1,0:T(8,128)(2,1)}, f32[2,80,512]{2,1,0:T(8,128)}, f32[2,80,512]{2,1,0:T(8,128)}) fusion(bf16[2,80,512]{2,1,0:T(8,128)(2,1)S(1)} %copy-done.6, f32[]{:T(128)} %bitcast.2, bf16[2,80,512]{2,1,0:T(8,128)(2,1)} %get-tuple-element.26, f32[2,80,512]{2,1,0:T(8,128)S(1)} %copy-done, f32[2,80,512]{2,1,0:T(8,128)S(1)} %copy-done.1), kind=kLoop, calls=%fused_computation.17 | loop fusion | flops 1392640 | bytes 1802244 | tf_op jit(solution)/shard_map/convert_element_type | solution.py:664
  207.3 0.0 copy-done.2
  207.3 0.0 copy-done.3
  207.3 0.0 copy-done.4
  207.3 0.0 copy-done.5
  207.3 0.0 copy-done.7
  207.4 0.0 copy-done.8
  207.4 3.0 %fusion.2 = (bf16[2,32,1280]{2,1,0:T(8,128)(2,1)}, f32[2,32,1280]{2,1,0:T(8,128)}, f32[2,32,1280]{2,1,0:T(8,128)}, bf16[2,32,1280]{2,1,0:T(8,128)(2,1)}, f32[2,32,1280]{2,1,0:T(8,128)}, /*index=5*/f32[2,32,1280]{2,1,0:T(8,128)}) fusion(bf16[2,32,1280]{2,1,0:T(8,128)(2,1)S(1)} %copy-done.7, f32[]{:T(128)} %bitcast.2, f32[2,32,1280]{2,1,0:T(8,128)S(1)} %copy-done.2, ...), kind=kLoop, calls=%fused_computation.11 | loop fusion | flops 2785280 | bytes 3604484 | tf_op jit(solution)/shard_map/convert_element_type | solution.py:664
Async XLA Ops:
  57.5 147.2 %copy-start = (f32[2,80,512]{2,1,0:T(8,128)S(1)}, f32[2,80,512]{2,1,0:T(8,128)}, u32[]{:S(2)}) copy-start(f32[2,80,512]{2,1,0:T(8,128)} %param.21) | copy-start | bytes 983044
  57.5 147.2 %copy-start.1 = (f32[2,80,512]{2,1,0:T(8,128)S(1)}, f32[2,80,512]{2,1,0:T(8,128)}, u32[]{:S(2)}) copy-start(f32[2,80,512]{2,1,0:T(8,128)} %param.18) | copy-start | bytes 983044
  57.5 147.2 %copy-start.6 = (bf16[2,80,512]{2,1,0:T(8,128)(2,1)S(1)}, bf16[2,80,512]{2,1,0:T(8,128)(2,1)}, u32[]{:S(2)}) copy-start(bf16[2,80,512]{2,1,0:T(8,128)(2,1)} %wd_ref.1) | copy-start | bytes 491524
  57.6 149.8 %copy-start.2 = (f32[2,32,1280]{2,1,0:T(8,128)S(1)}, f32[2,32,1280]{2,1,0:T(8,128)}, u32[]{:S(2)}) copy-start(f32[2,32,1280]{2,1,0:T(8,128)} %param.19) | copy-start | bytes 983044
  57.6 149.8 %copy-start.3 = (f32[2,32,1280]{2,1,0:T(8,128)S(1)}, f32[2,32,1280]{2,1,0:T(8,128)}, u32[]{:S(2)}) copy-start(f32[2,32,1280]{2,1,0:T(8,128)} %param.16) | copy-start | bytes 983044
  57.6 149.7 %copy-start.4 = (f32[2,32,1280]{2,1,0:T(8,128)S(1)}, f32[2,32,1280]{2,1,0:T(8,128)}, u32[]{:S(2)}) copy-start(f32[2,32,1280]{2,1,0:T(8,128)} %param.20) | copy-start | bytes 983044
  57.6 149.7 %copy-start.5 = (f32[2,32,1280]{2,1,0:T(8,128)S(1)}, f32[2,32,1280]{2,1,0:T(8,128)}, u32[]{:S(2)}) copy-start(f32[2,32,1280]{2,1,0:T(8,128)} %param.17) | copy-start | bytes 983044
  57.6 149.7 %copy-start.7 = (bf16[2,32,1280]{2,1,0:T(8,128)(2,1)S(1)}, bf16[2,32,1280]{2,1,0:T(8,128)(2,1)}, u32[]{:S(2)}) copy-start(bf16[2,32,1280]{2,1,0:T(8,128)(2,1)} %wg_ref.1) | copy-start | bytes 491524
  57.6 149.7 %copy-start.8 = (bf16[2,32,1280]{2,1,0:T(8,128)(2,1)S(1)}, bf16[2,32,1280]{2,1,0:T(8,128)(2,1)}, u32[]{:S(2)}) copy-start(bf16[2,32,1280]{2,1,0:T(8,128)(2,1)} %wu_ref.1) | copy-start | bytes 491524
where the time goes:
time: 211 us; the launch traced here: 210 us
  Pallas kernels  204 us (97%)
  other arithmetic  5.62 us (3%)
    pallas_call x1, Pallas kernels, backward(): pl.pallas_call(functools.partial(backward_kernel, n), out_shape=[jax.Shap...  147 us
    pallas_call x1, Pallas kernels, forward(): pl.pallas_call(functools.partial(forward_kernel, n), out_shape=[jax.Shape...  56.9 us
    convert_element_type x2, other arithmetic, adamw(): return ((w - 0.02 * step).astype(BF), m, v)  5.62 us

commit v1 on v0

--- a/solution.py
+++ b/solution.py
@@ -409,10 +409,12 @@
         return 2 * (q + q // nf)
 
     def events(p):
-        def each_gu(q, _):
-            s = p - (ready(q) + 2)
-
-            @pl.when(jnp.logical_and(s >= 0, s <= far))
+        def each_gu(k, _):
+            q = (p + 1) // 2 - far // 2 - 2 + k
+            s = p - (2 * q + 2)
+            s = s - 2 * jnp.where(q >= nf, 1, 0)
+
+            @pl.when(jnp.logical_and(jnp.logical_and(q >= 0, q < 2 * nf), jnp.logical_and(s >= 0, s <= far)))
             def _():
                 event(Gu(q), s)
 
@@ -431,7 +433,7 @@
         def _():
             lax.fori_loop(0, 2, each_d, 0)
 
-        lax.fori_loop(0, 2 * nf, each_gu, 0)
+        lax.fori_loop(0, far // 2 + 2, each_gu, 0)
 
     def grads(q):
         for b in range(nz):

time: 211 us -> 209 us (level)
  no operation moved by 1% of the time
where the time goes in v1:
time: 209 us
  Pallas kernels  202 us (97%)
  other arithmetic  5.62 us (3%)
    pallas_call x1, Pallas kernels, backward(): pl.pallas_call(functools.partial(backward_kernel, n), out_shape=[jax.Shap...  145 us
    pallas_call x1, Pallas kernels, forward(): pl.pallas_call(functools.partial(forward_kernel, n), out_shape=[jax.Shape...  56.9 us
    convert_element_type x2, other arithmetic, adamw(): return ((w - 0.02 * step).astype(BF), m, v)  5.62 us

profile of v1, /device:TPU:21, one launch (start us, length us, event | category | flops | bytes accessed | tf_op | source)
XLA Modules:
  0.0 208.7 jit_solution(6012138816299263818)
XLA Ops:
  0.6 56.9 %forward0.1 = (bf16[4096,512]{1,0:T(8,128)(2,1)}, bf16[4096,512]{1,0:T(8,128)(2,1)}, bf16[4096,1280]{1,0:T(8,128)(2,1)}, bf16[4096,512]{1,0:T(8,128)(2,1)}, bf16...) custom-call(bf16[4096,512]{1,0:T(8,128)(2,1)} %bitcast.25, bf16[2,32,1280]{2,1,0:T(8,128)(2,1)} %wg_ref.1, ...), custom_call_target="tpu_custom_call" | custom-call | flops 16106127360 | bytes 41943040 | tf_op jit(solution)/shard_map/forward0/pallas_call | solution.py:205
  57.5 0.0 copy-start
  57.5 0.0 copy-start.1
  57.5 0.0 copy-start.6
  57.6 0.0 copy-start.2
  57.6 0.0 copy-start.3
  57.6 0.0 copy-start.4
  57.6 0.0 copy-start.5
  57.6 0.0 copy-start.7
  57.6 0.0 copy-start.8
  57.6 145.3 %backward.1 = (bf16[2,2,32,1280]{3,2,1,0:T(8,128)(2,1)}, bf16[2,80,512]{2,1,0:T(8,128)(2,1)}, f32[1,1]{1,0:T(1,128)}) custom-call(bf16[4096,512]{1,0:T(8,128)(2,1)} %get-tuple-element.18.h1_hbm, bf16[4096,512]{1,0:T(8,128)(2,1)} %get-tuple-element.19.a1_hbm, bf16[4096,512]{1,0:T(8,128)(2,1)} %bitcast.26, bf16[4096,512]{1,0:T(8,128)(2,1)} %get-tuple-element.20.a0_hbm, ...), custom_call_target="tpu_custom_call" | custom-call | flops 75161927680 | bytes 41943040 | tf_op jit(solution)/shard_map/backward/pallas_call | solution.py:615
  203.0 0.0 copy-done
  203.0 0.0 copy-done.1
  203.0 0.0 copy-done.6
  203.0 2.6 %fusion.8 = (bf16[2,80,512]{2,1,0:T(8,128)(2,1)}, f32[2,80,512]{2,1,0:T(8,128)}, f32[2,80,512]{2,1,0:T(8,128)}) fusion(bf16[2,80,512]{2,1,0:T(8,128)(2,1)S(1)} %copy-done.6, f32[]{:T(128)} %bitcast.2, bf16[2,80,512]{2,1,0:T(8,128)(2,1)} %get-tuple-element.26, f32[2,80,512]{2,1,0:T(8,128)S(1)} %copy-done, f32[2,80,512]{2,1,0:T(8,128)S(1)} %copy-done.1), kind=kLoop, calls=%fused_computation.17 | loop fusion | flops 1392640 | bytes 1802244 | tf_op jit(solution)/shard_map/convert_element_type | solution.py:666
  205.6 0.0 copy-done.2
  205.6 0.0 copy-done.3
  205.6 0.0 copy-done.4
  205.6 0.0 copy-done.5
  205.6 0.0 copy-done.7
  205.6 0.0 copy-done.8
  205.6 3.0 %fusion.2 = (bf16[2,32,1280]{2,1,0:T(8,128)(2,1)}, f32[2,32,1280]{2,1,0:T(8,128)}, f32[2,32,1280]{2,1,0:T(8,128)}, bf16[2,32,1280]{2,1,0:T(8,128)(2,1)}, f32[2,32,1280]{2,1,0:T(8,128)}, /*index=5*/f32[2,32,1280]{2,1,0:T(8,128)}) fusion(bf16[2,32,1280]{2,1,0:T(8,128)(2,1)S(1)} %copy-done.7, f32[]{:T(128)} %bitcast.2, f32[2,32,1280]{2,1,0:T(8,128)S(1)} %copy-done.2, ...), kind=kLoop, calls=%fused_computation.11 | loop fusion | flops 2785280 | bytes 3604484 | tf_op jit(solution)/shard_map/convert_element_type | solution.py:666
Async XLA Ops:
  57.5 145.4 %copy-start = (f32[2,80,512]{2,1,0:T(8,128)S(1)}, f32[2,80,512]{2,1,0:T(8,128)}, u32[]{:S(2)}) copy-start(f32[2,80,512]{2,1,0:T(8,128)} %param.21) | copy-start | bytes 983044
  57.5 145.4 %copy-start.1 = (f32[2,80,512]{2,1,0:T(8,128)S(1)}, f32[2,80,512]{2,1,0:T(8,128)}, u32[]{:S(2)}) copy-start(f32[2,80,512]{2,1,0:T(8,128)} %param.18) | copy-start | bytes 983044
  57.5 145.4 %copy-start.6 = (bf16[2,80,512]{2,1,0:T(8,128)(2,1)S(1)}, bf16[2,80,512]{2,1,0:T(8,128)(2,1)}, u32[]{:S(2)}) copy-start(bf16[2,80,512]{2,1,0:T(8,128)(2,1)} %wd_ref.1) | copy-start | bytes 491524
  57.6 148.0 %copy-start.2 = (f32[2,32,1280]{2,1,0:T(8,128)S(1)}, f32[2,32,1280]{2,1,0:T(8,128)}, u32[]{:S(2)}) copy-start(f32[2,32,1280]{2,1,0:T(8,128)} %param.19) | copy-start | bytes 983044
  57.6 148.0 %copy-start.3 = (f32[2,32,1280]{2,1,0:T(8,128)S(1)}, f32[2,32,1280]{2,1,0:T(8,128)}, u32[]{:S(2)}) copy-start(f32[2,32,1280]{2,1,0:T(8,128)} %param.16) | copy-start | bytes 983044
  57.6 148.0 %copy-start.4 = (f32[2,32,1280]{2,1,0:T(8,128)S(1)}, f32[2,32,1280]{2,1,0:T(8,128)}, u32[]{:S(2)}) copy-start(f32[2,32,1280]{2,1,0:T(8,128)} %param.20) | copy-start | bytes 983044
  57.6 148.0 %copy-start.5 = (f32[2,32,1280]{2,1,0:T(8,128)S(1)}, f32[2,32,1280]{2,1,0:T(8,128)}, u32[]{:S(2)}) copy-start(f32[2,32,1280]{2,1,0:T(8,128)} %param.17) | copy-start | bytes 983044
  57.6 148.0 %copy-start.7 = (bf16[2,32,1280]{2,1,0:T(8,128)(2,1)S(1)}, bf16[2,32,1280]{2,1,0:T(8,128)(2,1)}, u32[]{:S(2)}) copy-start(bf16[2,32,1280]{2,1,0:T(8,128)(2,1)} %wg_ref.1) | copy-start | bytes 491524
  57.6 148.0 %copy-start.8 = (bf16[2,32,1280]{2,1,0:T(8,128)(2,1)S(1)}, bf16[2,32,1280]{2,1,0:T(8,128)(2,1)}, u32[]{:S(2)}) copy-start(bf16[2,32,1280]{2,1,0:T(8,128)(2,1)} %wu_ref.1) | copy-start | bytes 491524
